TPU v7x, 32 devices: a whole 2x2x4 slice. The times are simulated.
32 devices in a mesh: grp: 4 (over z), ctx: 2 (over y), wid: 4 (over x, core).
Axes of the slice: x: 2, y: 2, z: 4, core: 2. Of those that a mesh axis runs over, the one named last changes fastest.
Arguments:
- query: bfloat16 [256, 64, 128], P(None, 'wid'), may hold values from -64 to 64
- keys: bfloat16 [4, 512, 8, 128], P(None, ('grp', 'ctx'), 'wid'), may hold values from -64 to 64
- values: bfloat16 [4, 512, 8, 128], P(None, ('grp', 'ctx'), 'wid'), may hold values from -6 to 6
- lengths: int32 [4, 8], replicated, may hold values from 32 to 64
- query_pos: int32 [256], replicated, may hold values from 128 to 511
- resid: bfloat16 [256, 5120], P('wid', ('grp', 'ctx')), may hold values from -1.1953125 to 1.1953125
- out_weight: bfloat16 [8192, 5120], P('wid', ('grp', 'ctx')), may hold values from -0.0625 to 0.0625
- enc_weight: bfloat16 [5120, 24576], P('wid', ('grp', 'ctx')), may hold values from -0.078125 to 0.078125
- enc_bias: float32 [24576], P(('grp', 'ctx')), may hold values from -3 to 3
- dec_weight: bfloat16 [24576, 5120], P(('grp', 'ctx'), 'wid'), may hold values from -0.078125 to 0.078125
- dec_bias: float32 [5120], P('wid'), may hold values from -3 to 3
Outputs:
- layer_out: bfloat16 [256, 5120], P('wid', ('grp', 'ctx'))
- enc_grad: bfloat16 [5120, 24576], P('wid', ('grp', 'ctx'))
- enc_bias_grad: float32 [24576], P(('grp', 'ctx'))
- dec_grad: bfloat16 [24576, 5120], P(('grp', 'ctx'), 'wid')
- dec_bias_grad: float32 [5120], P('wid')
Inputs may be any that keep to these rules, and one draw needn't show every extreme that they name: `lengths`: live slots of a shard are its first ones.
All inputs are finite; a program needn't handle non-finite values.
Results may differ from a plain program's by a relative error of at most 0.024.
Values may be sent and summed in bfloat16 or wider, within the bound.
A program may use at most 128 MiB of HBM per device.

v0:
```python
import jax
import jax.numpy as jnp
from jax import lax
from jax.sharding import PartitionSpec as P

HD = 128


def body(
    query,
    keys,
    values,
    lengths,
    query_pos,
    resid,
    out_weight,
    enc_weight,
    enc_bias,
    dec_weight,
    dec_bias,
):
    seq_count, slot_count, kv_local, head_dim = keys.shape
    row_count = query.shape[0]
    heads_local = query.shape[1]
    group_size = heads_local // kv_local
    rows_each = row_count // seq_count
    shard_pos = lax.axis_index(("grp", "ctx"))
    shard_ids = jnp.arange(lengths.shape[1], dtype=jnp.int32)
    offset = jnp.sum(jnp.where(shard_ids[None, :] < shard_pos, lengths, 0), axis=1)
    live_count = jnp.sum(jnp.where(shard_ids[None, :] == shard_pos, lengths, 0), axis=1)
    slot_ids = jnp.arange(slot_count, dtype=jnp.int32)
    key_pos = offset[:, None] + slot_ids[None, :]
    live_slot = slot_ids[None, :] < live_count[:, None]
    row_position = query_pos.reshape(seq_count, rows_each)
    visible = live_slot[:, None, :] & (key_pos[:, None, :] <= row_position[:, :, None])
    visible_mask = visible[:, :, None, None, :]
    q_view = query.reshape(seq_count, rows_each, kv_local, group_size, head_dim)
    scores = jnp.einsum(
        "srkgd,sjkd->srkgj", q_view, keys, preferred_element_type=jnp.float32
    ) * HD ** (-0.5)
    local_peak = jnp.max(jnp.where(visible_mask, scores, -1e30), axis=-1)
    peak = lax.pmax(local_peak, ("grp", "ctx"))
    weights = jnp.where(visible_mask, jnp.exp(scores - peak[..., None]), 0.0)
    weight_sum = jnp.sum(weights, axis=-1)
    weights_low = weights.astype(jnp.bfloat16)
    weighted = jnp.einsum(
        "srkgj,sjkd->srkgd", weights_low, values, preferred_element_type=jnp.float32
    )
    weight_sum, weighted = (weight_sum, weighted)
    weight_sum, weighted = lax.psum((weight_sum, weighted), ("grp", "ctx"))
    attention = (weighted / weight_sum[..., None]).astype(jnp.bfloat16)
    attention = attention.reshape(row_count, heads_local * head_dim)
    projected = jnp.dot(attention, out_weight, preferred_element_type=jnp.float32)
    mixed = lax.psum_scatter(
        projected.astype(jnp.bfloat16), "wid", scatter_dimension=0, tiled=True
    ).astype(jnp.float32)
    layer_out = (mixed + resid.astype(jnp.float32)).astype(jnp.bfloat16)
    wide_rows = lax.all_gather(layer_out, ("grp", "ctx"), axis=1, tiled=True)
    block = lax.all_to_all(wide_rows, "wid", split_axis=1, concat_axis=0, tiled=True)
    enc_part = jnp.dot(block, enc_weight, preferred_element_type=jnp.float32)
    preact = lax.psum(enc_part.astype(jnp.bfloat16), "wid").astype(jnp.float32) + enc_bias
    latents = (jax.nn.softplus(4.0 * preact) * 0.25).astype(jnp.bfloat16)
    row_scale = row_count ** (-0.5)
    recon = lax.psum_scatter(
        jnp.dot(latents, dec_weight, preferred_element_type=jnp.float32),
        ("grp", "ctx"),
        scatter_dimension=0,
        tiled=True,
    )
    piece_len = recon.shape[0]
    target = lax.dynamic_slice_in_dim(block, shard_pos * piece_len, piece_len, 0).astype(
        jnp.float32
    )
    scaled_error = ((recon + dec_bias - target) * row_scale).astype(jnp.bfloat16)
    error_all = lax.all_gather(scaled_error, ("grp", "ctx"), axis=0, tiled=True)
    dec_bias_grad = jnp.sum(error_all, axis=0, dtype=jnp.float32)
    latent_part = lax.dot_general(
        error_all, dec_weight, (((1,), (1,)), ((), ())), preferred_element_type=jnp.float32
    )
    dec_grad = lax.dot_general(
        latents, error_all, (((0,), (0,)), ((), ())), preferred_element_type=jnp.float32
    )
    latent_grad = lax.psum(latent_part.astype(jnp.bfloat16), "wid").astype(jnp.float32)
    preact_grad = (latent_grad * jax.nn.sigmoid(4.0 * preact)).astype(jnp.bfloat16)
    enc_grad = lax.dot_general(
        block, preact_grad, (((0,), (0,)), ((), ())), preferred_element_type=jnp.float32
    ).astype(jnp.bfloat16)
    enc_bias_grad = jnp.sum(preact_grad, axis=0, dtype=jnp.float32)
    return (layer_out, enc_grad, enc_bias_grad, dec_grad.astype(jnp.bfloat16), dec_bias_grad)


def solution(mesh):
    placed = (
        P(None, "wid", None),
        P(None, ("grp", "ctx"), "wid", None),
        P(None, ("grp", "ctx"), "wid", None),
        P(),
        P(),
        P("wid", ("grp", "ctx")),
        P("wid", ("grp", "ctx")),
        P("wid", ("grp", "ctx")),
        P(("grp", "ctx")),
        P(("grp", "ctx"), "wid"),
        P("wid"),
    )
    return jax.shard_map(
        body,
        mesh=mesh,
        in_specs=placed,
        out_specs=(
            P("wid", ("grp", "ctx")),
            P("wid", ("grp", "ctx")),
            P(("grp", "ctx")),
            P(("grp", "ctx"), "wid"),
            P("wid"),
        ),
        check_vma=False,
    )
```

profile of v0, /device:TPU:0, one launch (start us, length us, event | category | flops | bytes accessed | tf_op | source)
XLA Modules:
  0.0 456.0 jit_solution(1669517848478432027)
XLA Ops:
  7.2 0.0 copy-start
  7.2 0.0 all-reduce.4.cloned.1.call-start
  7.2 0.9 le.20
  8.1 0.8 select_reduce_fusion.1
  9.0 0.1 iota_add_fusion
  9.0 0.1 iota_compare_fusion
  9.1 0.1 compare_and_fusion
  9.3 3.8 fusion.2
  13.0 0.0 copy-start.3
  13.0 39.0 %pmax.7 = f32[4,64,2,8]{1,3,2,0:T(8,128)S(1)} all-reduce(f32[4,64,2,8]{1,3,2,0:T(8,128)S(1)} %get-tuple-element.11), channel_id=1, replica_groups=mesh['grp'=4,'ctx'=2,'wid'=4] {'grp','ctx'}, use_global_device_ids=true, to_apply=%region_3.4 | all-reduce | flops 4096 | bytes 32768 | tf_op jit(solution)/shard_map/pmax | solution.py:42
  52.0 3.2 fusion.5
  55.3 2.4 copy.29
  57.7 0.0 copy-done.3
  57.7 3.0 convolution_bitcast_fusion
  60.6 0.0 all-reduce.4.cloned.1.call-update
  60.7 0.0 reduce-scatter.3.cloned.1.call-start
  60.7 34.2 %psum.29 = f32[4,64,2,8]{1,3,2,0:T(8,128)S(1)} all-reduce(f32[4,64,2,8]{1,3,2,0:T(8,128)S(1)} %get-tuple-element.9), channel_id=1, replica_groups=mesh['grp'=4,'ctx'=2,'wid'=4] {'grp','ctx'}, use_global_device_ids=true, to_apply=%region_6.7 | all-reduce | flops 4096 | bytes 32768 | tf_op jit(solution)/shard_map/psum | solution.py:50
  94.9 0.1 copy.31
  95.0 65.7 %all-reduce.4.cloned.1.call-done = f32[4,64,2,8,128]{4,3,1,2,0:T(8,128)} async-done(((f32[4,64,2,8,128]{4,3,1,2,0:T(8,128)}), f32[4,64,2,8,128]{4,3,1,2,0:T(8,128)}) %all-reduce.4.cloned.1.call-update) | async-done | bytes 2097168 | tf_op jit(solution)/shard_map/psum | solution.py:50
  160.8 1.9 divide_convert_fusion
  162.7 1.2 copy.32
  163.9 0.0 copy-start.4
  163.9 2.3 reshape.71
  166.2 0.0 copy-done
  166.2 2.9 convolution_convert_fusion.4
  169.1 0.0 reduce-scatter.3.cloned.1.call-update
  169.1 0.0 all-reduce.6.cloned.1.call-start
  169.2 19.8 %reduce-scatter.3.cloned.1.call-done = bf16[64,640]{1,0:T(8,128)(2,1)} async-done(((bf16[256,640]{1,0:T(8,128)(2,1)}), bf16[64,640]{1,0:T(8,128)(2,1)}) %reduce-scatter.3.cloned.1.call-update) | async-done | bytes 81936 | tf_op jit(solution)/shard_map/reduce_scatter | solution.py:54
  189.0 0.0 copy-done.4
  189.0 0.9 add_convert_fusion
  189.9 0.0 copy-start.2
  189.9 32.1 %all_gather.6 = bf16[64,5120]{1,0:T(8,128)(2,1)S(1)} all-gather(bf16[64,640]{1,0:T(8,128)(2,1)S(1)} %add_convert_fusion), channel_id=1, replica_groups=mesh['grp'=4,'ctx'=2,'wid'=4] {'grp','ctx'}, dimensions={1}, use_global_device_ids=true | all-gather | bytes 737280 | tf_op jit(solution)/shard_map/all_gather | solution.py:58
  222.1 12.6 %all_to_all.19 = bf16[64,4,1280]{2,0,1:T(8,128)(2,1)S(1)} all-to-all(bf16[64,4,1280]{2,0,1:T(8,128)(2,1)S(1)} %bitcast.41), channel_id=1, replica_groups=mesh['grp'=4,'ctx'=2,'wid'=4] {'wid'}, dimensions={1} | all-to-all | bytes 1310720 | tf_op jit(solution)/shard_map/all_to_all | solution.py:59
  234.7 0.0 copy-start.5
  234.7 6.6 %convolution_convert_fusion.3 = bf16[256,3072]{1,0:T(8,128)(2,1)} fusion(bf16[256,1280]{1,0:T(8,128)(2,1)S(1)} %bitcast.38, bf16[1280,3072]{1,0:T(8,128)(2,1)} %param.18), kind=kOutput, calls=%fused_computation.4 | convolution fusion | flops 2014052352 | bytes 10092544 | tf_op jit(solution)/shard_map/dot_general | solution.py:60
  241.3 0.0 copy-done.2
  241.3 0.0 all-reduce.6.cloned.1.call-update
  241.4 0.0 copy-start.6
  241.4 0.0 reduce-scatter.5.cloned.1.call-start
  241.4 42.7 %all-reduce.6.cloned.1.call-done = bf16[256,3072]{1,0:T(8,128)(2,1)} async-done(((bf16[256,3072]{1,0:T(8,128)(2,1)}), bf16[256,3072]{1,0:T(8,128)(2,1)}) %all-reduce.6.cloned.1.call-update) | async-done | bytes 1572880 | tf_op jit(solution)/shard_map/psum | solution.py:61
  284.1 0.0 copy-done.5
  284.1 8.8 %fusion.12 = f32[256,1280]{1,0:T(8,128)} fusion(bf16[3072,1280]{1,0:T(8,128)(2,1)} %param.20, bf16[256,3072]{1,0:T(8,128)(2,1)} %all-reduce.6.cloned.1.call-done, f32[3072]{0:T(1024)S(1)} %copy-done.5), kind=kOutput, calls=%fused_computation.35 | convolution fusion | flops 2021916672 | bytes 10760192 | tf_op jit(solution)/shard_map/dot_general | solution.py:65
  292.9 0.0 reduce-scatter.5.cloned.1.call-update
  293.0 0.0 all-reduce.8.cloned.1.call-start
  293.0 65.3 %reduce-scatter.5.cloned.1.call-done = f32[32,1280]{1,0:T(8,128)} async-done(((f32[256,1280]{1,0:T(8,128)}), f32[32,1280]{1,0:T(8,128)}) %reduce-scatter.5.cloned.1.call-update) | async-done | bytes 163856 | tf_op jit(solution)/shard_map/reduce_scatter | solution.py:64
  358.3 0.0 copy-done.6
  358.3 0.9 multiply_convert_fusion.1
  359.2 32.1 %all_gather.7 = bf16[256,1280]{1,0:T(8,128)(2,1)S(1)} all-gather(bf16[32,1280]{1,0:T(8,128)(2,1)S(1)} %multiply_convert_fusion.1), channel_id=1, replica_groups=mesh['grp'=4,'ctx'=2,'wid'=4] {'grp','ctx'}, dimensions={0}, use_global_device_ids=true | all-gather | bytes 737280 | tf_op jit(solution)/shard_map/all_gather | solution.py:75
  391.4 0.0 copy-start.1
  391.4 0.8 copy-done.1
  392.2 6.6 %convolution_convert_fusion.2 = bf16[256,3072]{1,0:T(8,128)(2,1)} fusion(bf16[256,1280]{1,0:T(8,128)(2,1)S(1)} %all_gather.7, bf16[3072,1280]{1,0:T(8,128)(2,1)} %param.20), kind=kOutput, calls=%fused_computation.3 | convolution fusion | flops 2014052352 | bytes 10092544 | tf_op jit(solution)/shard_map/dot_general | solution.py:77
  398.8 0.0 all-reduce.8.cloned.1.call-update
  398.8 1.8 convert_reduce_fusion.1
  400.6 9.0 %convolution_convert_fusion = bf16[3072,1280]{1,0:T(8,128)(2,1)} fusion(bf16[256,1280]{1,0:T(8,128)(2,1)} %copy-done.1, bf16[256,3072]{1,0:T(8,128)(2,1)} %all-reduce.6.cloned.1.call-done, f32[3072]{0:T(1024)S(1)} %copy-done.5), kind=kOutput, calls=%fused_computation | convolution fusion | flops 2025848832 | bytes 10104832 | tf_op jit(solution)/shard_map/dot_general | solution.py:80
  409.6 30.8 %all-reduce.8.cloned.1.call-done = bf16[256,3072]{1,0:T(8,128)(2,1)} async-done(((bf16[256,3072]{1,0:T(8,128)(2,1)}), bf16[256,3072]{1,0:T(8,128)(2,1)}) %all-reduce.8.cloned.1.call-update) | async-done | bytes 1572880 | tf_op jit(solution)/shard_map/psum | solution.py:83
  440.4 3.6 convert_reduce_fusion
  444.0 5.5 %convolution_convert_fusion.1 = bf16[1280,3072]{1,0:T(8,128)(2,1)} fusion(bf16[256,1280]{1,0:T(8,128)(2,1)S(1)} %bitcast.40, bf16[256,3072]{1,0:T(8,128)(2,1)S(1)} %get-tuple-element.8), kind=kOutput, calls=%fused_computation.1 | convolution fusion | flops 2017198080 | bytes 10092544 | tf_op jit(solution)/shard_map/dot_general | solution.py:85
  (2 shorter events, 0.0 us)
Async XLA Ops:
  7.2 159.0 %copy-start = (bf16[2048,640]{1,0:T(8,128)(2,1)S(1)}, bf16[2048,640]{1,0:T(8,128)(2,1)}, u32[]{:S(2)}) copy-start(bf16[2048,640]{1,0:T(8,128)(2,1)} %param.17) | copy-start | bytes 7864324
  7.2 153.6 %all-reduce.4.cloned.1.call-start = ((), (), s32[]{:S(2)}) async-start(), calls=%async_computation.3 | async-start | bytes 4194304 | tf_op jit(solution)/shard_map/psum | solution.py:50
  13.0 44.6 %copy-start.3 = (bf16[4,64,2,128]{3,2,1,0:T(2,128)(2,1)S(1)}, bf16[4,64,2,128]{3,2,1,0:T(2,128)(2,1)}, u32[]{:S(2)}) copy-start(bf16[4,64,2,128]{3,2,1,0:T(2,128)(2,1)} %param.13) | copy-start | bytes 393220
  60.7 128.4 %reduce-scatter.3.cloned.1.call-start = ((), (), s32[]{:S(2)}) async-start(), calls=%async_computation.4 | async-start | bytes 409600 | tf_op jit(solution)/shard_map/reduce_scatter | solution.py:54
  163.9 25.1 %copy-start.4 = (bf16[64,640]{1,0:T(8,128)(2,1)S(1)}, bf16[64,640]{1,0:T(8,128)(2,1)}, u32[]{:S(2)}) copy-start(bf16[64,640]{1,0:T(8,128)(2,1)} %param.16) | copy-start | bytes 245764
  169.1 114.9 %all-reduce.6.cloned.1.call-start = ((), (), s32[]{:S(2)}) async-start(), calls=%async_computation.5 | async-start | bytes 3145728 | tf_op jit(solution)/shard_map/psum | solution.py:61
  189.9 51.4 %copy-start.2 = (bf16[64,640]{1,0:T(8,128)(2,1)}, bf16[64,640]{1,0:T(8,128)(2,1)S(1)}, u32[]{:S(2)}) copy-start(bf16[64,640]{1,0:T(8,128)(2,1)S(1)} %add_convert_fusion) | copy-start | bytes 245764
  234.7 49.3 %copy-start.5 = (f32[3072]{0:T(1024)S(1)}, f32[3072]{0:T(1024)}, u32[]{:S(2)}) copy-start(f32[3072]{0:T(1024)} %param.19) | copy-start | bytes 36868
  241.4 116.9 %copy-start.6 = (f32[1280]{0:T(1024)S(1)}, f32[1280]{0:T(1024)}, u32[]{:S(2)}) copy-start(f32[1280]{0:T(1024)} %param.21) | copy-start | bytes 15364
  241.4 116.9 %reduce-scatter.5.cloned.1.call-start = ((), (), s32[]{:S(2)}) async-start(), calls=%async_computation.6 | async-start | bytes 1474560 | tf_op jit(solution)/shard_map/reduce_scatter | solution.py:64
  293.0 147.5 %all-reduce.8.cloned.1.call-start = ((), (), s32[]{:S(2)}) async-start(), calls=%async_computation.7 | async-start | bytes 3145728 | tf_op jit(solution)/shard_map/psum | solution.py:83
  391.4 0.8 copy-start.1
Sparse Core Ops, SparseCore 0:
  60.8 99.9 all-reduce.3
  169.3 19.6 reduce-scatter.2
  241.5 42.5 all-reduce.5
  293.1 65.1 reduce-scatter.4
  398.9 41.4 all-reduce.7
where the time goes:
time: 457 us; the launch traced here: 456 us
  waiting for transfers between devices  224 us (49%)
  blocking collectives  150 us (33%)
  matrix products  46.2 us (10%)
  between operations  13.9 us (3%)
  other arithmetic  13.5 us (3%)
  local copies, waits for them, and re-layouts  7.82 us (2%)
    psum x1, waiting for transfers between devices, body(): weight_sum, weighted = lax.psum((weight_sum, weighted), ('grp', 'ctx'))  65.7 us
    reduce_scatter x1, waiting for transfers between devices, body(): lax.psum_scatter(jnp.dot(latents, dec_weight, preferred_element_type=jnp....  65.3 us
    psum x1, waiting for transfers between devices, body(): lax.psum(enc_part.astype(jnp.bfloat16), 'wid').astype(jnp.float32)  42.7 us
    pmax x1, blocking collectives, body(): peak = lax.pmax(local_peak, ('grp', 'ctx'))  39 us
    psum x1, blocking collectives, body(): weight_sum, weighted = lax.psum((weight_sum, weighted), ('grp', 'ctx'))  34.2 us
    all_gather x1, blocking collectives, body(): wide_rows = lax.all_gather(layer_out, ('grp', 'ctx'), axis=1, tiled=True)  32.1 us
    all_gather x1, blocking collectives, body(): error_all = lax.all_gather(scaled_error, ('grp', 'ctx'), axis=0, tiled=True)  32.1 us
    psum x1, waiting for transfers between devices, body(): lax.psum(latent_part.astype(jnp.bfloat16), 'wid').astype(jnp.float32)  30.8 us
  transfers between devices with their start and end apart: 5, of which 5 were waited for; matrix products, arithmetic and copies ran while one was open for 2% of the time, Pallas kernels for 0%

commit v1 on v0

--- a/solution.py
+++ b/solution.py
@@ -47,7 +47,7 @@
         "srkgj,sjkd->srkgd", weights_low, values, preferred_element_type=jnp.float32
     )
     weight_sum, weighted = (weight_sum, weighted)
-    weight_sum, weighted = lax.psum((weight_sum, weighted), ("grp", "ctx"))
+    weight_sum, weighted = lax.psum(lax.psum((weight_sum, weighted), "ctx"), "grp")
     attention = (weighted / weight_sum[..., None]).astype(jnp.bfloat16)
     attention = attention.reshape(row_count, heads_local * head_dim)
     projected = jnp.dot(attention, out_weight, preferred_element_type=jnp.float32)

time: 457 us -> 506 us (1.11)
  waiting for transfers between devices: 224 us -> 280 us
  blocking collectives: 150 us -> 144 us
    psum x1 -> x2, waiting for transfers between devices: 65.7 us -> 122 us  [the longest x1 61.2 us: body(): lax.psum(lax.psum((weight_sum, weighted), 'ctx'), 'grp')]
    psum x1 -> x2, blocking collectives: 34.2 us -> 28.1 us  [the longest x1 20.9 us: body(): lax.psum(lax.psum((weight_sum, weighted), 'ctx'), 'grp')]
  transfers between devices with their start and end apart: 5 -> 6, of which waited for: 5 -> 6; matrix products, arithmetic and copies ran while one was open for 2% -> 2% of each run, Pallas kernels for 0% -> 0%
where the time goes in v1:
time: 506 us
  waiting for transfers between devices  280 us (55%)
  blocking collectives  144 us (28%)
  matrix products  46.2 us (9%)
  between operations  14.2 us (3%)
  other arithmetic  13.5 us (3%)
  local copies, waits for them, and re-layouts  7.82 us (2%)
    reduce_scatter x1, waiting for transfers between devices, body(): lax.psum_scatter(jnp.dot(latents, dec_weight, preferred_element_type=jnp....  65.3 us
    psum x1, waiting for transfers between devices, body(): lax.psum(lax.psum((weight_sum, weighted), 'ctx'), 'grp')  61.2 us
    psum x1, waiting for transfers between devices, body(): lax.psum((weight_sum, weighted), 'ctx')  60.3 us
    psum x1, waiting for transfers between devices, body(): lax.psum(enc_part.astype(jnp.bfloat16), 'wid').astype(jnp.float32)  42.8 us
    pmax x1, blocking collectives, body(): peak = lax.pmax(local_peak, ('grp', 'ctx'))  39 us
    all_gather x1, blocking collectives, body(): error_all = lax.all_gather(scaled_error, ('grp', 'ctx'), axis=0, tiled=True)  32.1 us
    all_gather x1, blocking collectives, body(): wide_rows = lax.all_gather(layer_out, ('grp', 'ctx'), axis=1, tiled=True)  31.9 us
    psum x1, waiting for transfers between devices, body(): lax.psum(latent_part.astype(jnp.bfloat16), 'wid').astype(jnp.float32)  30.8 us
  transfers between devices with their start and end apart: 6, of which 6 were waited for; matrix products, arithmetic and copies ran while one was open for 2% of the time, Pallas kernels for 0%

profile of v1, /device:TPU:0, one launch (start us, length us, event | category | flops | bytes accessed | tf_op | source)
XLA Modules:
  0.0 505.8 jit_solution(15836870261231741317)
XLA Ops:
  7.2 0.0 copy-start
  7.2 0.0 all-reduce.5.cloned.1.call-start
  7.2 0.9 le.20
  8.1 0.8 select_reduce_fusion.1
  9.0 0.1 iota_add_fusion
  9.0 0.1 iota_compare_fusion
  9.1 0.1 compare_and_fusion
  9.3 3.8 fusion.2
  13.0 0.0 copy-start.3
  13.0 39.0 %pmax.7 = f32[4,64,2,8]{1,3,2,0:T(8,128)S(1)} all-reduce(f32[4,64,2,8]{1,3,2,0:T(8,128)S(1)} %get-tuple-element.11), channel_id=1, replica_groups=mesh['grp'=4,'ctx'=2,'wid'=4] {'grp','ctx'}, use_global_device_ids=true, to_apply=%region_3.4 | all-reduce | flops 4096 | bytes 32768 | tf_op jit(solution)/shard_map/pmax | solution.py:42
  52.0 3.2 fusion.5
  55.3 2.4 copy.29
  57.7 0.0 copy-done.3
  57.7 3.0 convolution_bitcast_fusion
  60.6 0.0 all-reduce.5.cloned.1.call-update
  60.7 0.0 all-reduce.7.cloned.1.call-start
  60.7 60.3 %all-reduce.5.cloned.1.call-done = f32[4,64,2,8,128]{4,3,1,2,0:T(8,128)} async-done(((f32[4,64,2,8,128]{4,3,1,2,0:T(8,128)}), f32[4,64,2,8,128]{4,3,1,2,0:T(8,128)}) %all-reduce.5.cloned.1.call-update) | async-done | bytes 2097168 | tf_op jit(solution)/shard_map/psum | solution.py:50
  121.0 0.0 all-reduce.7.cloned.1.call-update
  121.1 0.0 reduce-scatter.3.cloned.1.call-start
  121.1 7.2 %psum.44 = f32[4,64,2,8]{1,3,2,0:T(8,128)S(1)} all-reduce(f32[4,64,2,8]{1,3,2,0:T(8,128)S(1)} %get-tuple-element.9), channel_id=1, replica_groups=mesh['grp'=4,'ctx'=2,'wid'=4] {'ctx'}, use_global_device_ids=true, to_apply=%region_7.8 | all-reduce | flops 4096 | bytes 32768 | tf_op jit(solution)/shard_map/psum | solution.py:50
  128.3 20.9 %psum.45 = f32[4,64,2,8]{1,3,2,0:T(8,128)S(1)} all-reduce(f32[4,64,2,8]{1,3,2,0:T(8,128)S(1)} %psum.44), channel_id=1, replica_groups=mesh['grp'=4,'ctx'=2,'wid'=4] {'grp'}, use_global_device_ids=true, to_apply=%region_8.9 | all-reduce | flops 4096 | bytes 32768 | tf_op jit(solution)/shard_map/psum | solution.py:50
  149.2 0.1 copy.31
  149.4 61.2 %all-reduce.7.cloned.1.call-done = f32[4,64,2,8,128]{4,3,1,2,0:T(8,128)} async-done(((f32[4,64,2,8,128]{4,3,1,2,0:T(8,128)}), f32[4,64,2,8,128]{4,3,1,2,0:T(8,128)}) %all-reduce.7.cloned.1.call-update) | async-done | bytes 2097168 | tf_op jit(solution)/shard_map/psum | solution.py:50
  210.6 1.9 divide_convert_fusion
  212.5 1.2 copy.32
  213.7 0.0 copy-start.4
  213.7 2.3 reshape.71
  216.0 0.0 copy-done
  216.0 2.9 convolution_convert_fusion.4
  218.9 0.0 reduce-scatter.3.cloned.1.call-update
  218.9 0.0 all-reduce.9.cloned.1.call-start
  219.0 19.6 %reduce-scatter.3.cloned.1.call-done = bf16[64,640]{1,0:T(8,128)(2,1)} async-done(((bf16[256,640]{1,0:T(8,128)(2,1)}), bf16[64,640]{1,0:T(8,128)(2,1)}) %reduce-scatter.3.cloned.1.call-update) | async-done | bytes 81936 | tf_op jit(solution)/shard_map/reduce_scatter | solution.py:54
  238.5 0.0 copy-done.4
  238.5 0.9 add_convert_fusion
  239.5 0.0 copy-start.2
  239.5 31.9 %all_gather.6 = bf16[64,5120]{1,0:T(8,128)(2,1)S(1)} all-gather(bf16[64,640]{1,0:T(8,128)(2,1)S(1)} %add_convert_fusion), channel_id=1, replica_groups=mesh['grp'=4,'ctx'=2,'wid'=4] {'grp','ctx'}, dimensions={1}, use_global_device_ids=true | all-gather | bytes 737280 | tf_op jit(solution)/shard_map/all_gather | solution.py:58
  271.4 12.6 %all_to_all.19 = bf16[64,4,1280]{2,0,1:T(8,128)(2,1)S(1)} all-to-all(bf16[64,4,1280]{2,0,1:T(8,128)(2,1)S(1)} %bitcast.41), channel_id=1, replica_groups=mesh['grp'=4,'ctx'=2,'wid'=4] {'wid'}, dimensions={1} | all-to-all | bytes 1310720 | tf_op jit(solution)/shard_map/all_to_all | solution.py:59
  284.1 0.0 copy-start.5
  284.1 6.6 %convolution_convert_fusion.3 = bf16[256,3072]{1,0:T(8,128)(2,1)} fusion(bf16[256,1280]{1,0:T(8,128)(2,1)S(1)} %bitcast.38, bf16[1280,3072]{1,0:T(8,128)(2,1)} %param.18), kind=kOutput, calls=%fused_computation.4 | convolution fusion | flops 2014052352 | bytes 10092544 | tf_op jit(solution)/shard_map/dot_general | solution.py:60
  290.6 0.0 copy-done.2
  290.6 0.0 all-reduce.9.cloned.1.call-update
  290.7 0.0 copy-start.6
  290.7 0.0 reduce-scatter.5.cloned.1.call-start
  290.7 42.8 %all-reduce.9.cloned.1.call-done = bf16[256,3072]{1,0:T(8,128)(2,1)} async-done(((bf16[256,3072]{1,0:T(8,128)(2,1)}), bf16[256,3072]{1,0:T(8,128)(2,1)}) %all-reduce.9.cloned.1.call-update) | async-done | bytes 1572880 | tf_op jit(solution)/shard_map/psum | solution.py:61
  333.6 0.0 copy-done.5
  333.6 8.8 %fusion.12 = f32[256,1280]{1,0:T(8,128)} fusion(bf16[3072,1280]{1,0:T(8,128)(2,1)} %param.20, bf16[256,3072]{1,0:T(8,128)(2,1)} %all-reduce.9.cloned.1.call-done, f32[3072]{0:T(1024)S(1)} %copy-done.5), kind=kOutput, calls=%fused_computation.35 | convolution fusion | flops 2021916672 | bytes 10760192 | tf_op jit(solution)/shard_map/dot_general | solution.py:65
  342.4 0.0 reduce-scatter.5.cloned.1.call-update
  342.4 0.0 all-reduce.11.cloned.1.call-start
  342.5 65.3 %reduce-scatter.5.cloned.1.call-done = f32[32,1280]{1,0:T(8,128)} async-done(((f32[256,1280]{1,0:T(8,128)}), f32[32,1280]{1,0:T(8,128)}) %reduce-scatter.5.cloned.1.call-update) | async-done | bytes 163856 | tf_op jit(solution)/shard_map/reduce_scatter | solution.py:64
  407.8 0.0 copy-done.6
  407.8 0.9 multiply_convert_fusion.1
  408.7 32.1 %all_gather.7 = bf16[256,1280]{1,0:T(8,128)(2,1)S(1)} all-gather(bf16[32,1280]{1,0:T(8,128)(2,1)S(1)} %multiply_convert_fusion.1), channel_id=1, replica_groups=mesh['grp'=4,'ctx'=2,'wid'=4] {'grp','ctx'}, dimensions={0}, use_global_device_ids=true | all-gather | bytes 737280 | tf_op jit(solution)/shard_map/all_gather | solution.py:75
  440.8 0.0 copy-start.1
  440.8 0.8 copy-done.1
  441.7 6.6 %convolution_convert_fusion.2 = bf16[256,3072]{1,0:T(8,128)(2,1)} fusion(bf16[256,1280]{1,0:T(8,128)(2,1)S(1)} %all_gather.7, bf16[3072,1280]{1,0:T(8,128)(2,1)} %param.20), kind=kOutput, calls=%fused_computation.3 | convolution fusion | flops 2014052352 | bytes 10092544 | tf_op jit(solution)/shard_map/dot_general | solution.py:77
  448.3 0.0 all-reduce.11.cloned.1.call-update
  448.3 1.8 convert_reduce_fusion.1
  450.1 9.0 %convolution_convert_fusion = bf16[3072,1280]{1,0:T(8,128)(2,1)} fusion(bf16[256,1280]{1,0:T(8,128)(2,1)} %copy-done.1, bf16[256,3072]{1,0:T(8,128)(2,1)} %all-reduce.9.cloned.1.call-done, f32[3072]{0:T(1024)S(1)} %copy-done.5), kind=kOutput, calls=%fused_computation | convolution fusion | flops 2025848832 | bytes 10104832 | tf_op jit(solution)/shard_map/dot_general | solution.py:80
  459.1 30.8 %all-reduce.11.cloned.1.call-done = bf16[256,3072]{1,0:T(8,128)(2,1)} async-done(((bf16[256,3072]{1,0:T(8,128)(2,1)}), bf16[256,3072]{1,0:T(8,128)(2,1)}) %all-reduce.11.cloned.1.call-update) | async-done | bytes 1572880 | tf_op jit(solution)/shard_map/psum | solution.py:83
  489.9 3.6 convert_reduce_fusion
  493.5 5.5 %convolution_convert_fusion.1 = bf16[1280,3072]{1,0:T(8,128)(2,1)} fusion(bf16[256,1280]{1,0:T(8,128)(2,1)S(1)} %bitcast.40, bf16[256,3072]{1,0:T(8,128)(2,1)S(1)} %get-tuple-element.8), kind=kOutput, calls=%fused_computation.1 | convolution fusion | flops 2017198080 | bytes 10092544 | tf_op jit(solution)/shard_map/dot_general | solution.py:85
  (2 shorter events, 0.0 us)
Async XLA Ops:
  7.2 208.8 %copy-start = (bf16[2048,640]{1,0:T(8,128)(2,1)S(1)}, bf16[2048,640]{1,0:T(8,128)(2,1)}, u32[]{:S(2)}) copy-start(bf16[2048,640]{1,0:T(8,128)(2,1)} %param.17) | copy-start | bytes 7864324
  7.2 113.9 %all-reduce.5.cloned.1.call-start = ((), (), s32[]{:S(2)}) async-start(), calls=%async_computation.3 | async-start | bytes 4194304 | tf_op jit(solution)/shard_map/psum | solution.py:50
  13.0 44.6 %copy-start.3 = (bf16[4,64,2,128]{3,2,1,0:T(2,128)(2,1)S(1)}, bf16[4,64,2,128]{3,2,1,0:T(2,128)(2,1)}, u32[]{:S(2)}) copy-start(bf16[4,64,2,128]{3,2,1,0:T(2,128)(2,1)} %param.13) | copy-start | bytes 393220
  60.7 149.9 %all-reduce.7.cloned.1.call-start = ((), (), s32[]{:S(2)}) async-start(), calls=%async_computation.4 | async-start | bytes 4194304 | tf_op jit(solution)/shard_map/psum | solution.py:50
  121.1 117.5 %reduce-scatter.3.cloned.1.call-start = ((), (), s32[]{:S(2)}) async-start(), calls=%async_computation.5 | async-start | bytes 409600 | tf_op jit(solution)/shard_map/reduce_scatter | solution.py:54
  213.7 24.9 %copy-start.4 = (bf16[64,640]{1,0:T(8,128)(2,1)S(1)}, bf16[64,640]{1,0:T(8,128)(2,1)}, u32[]{:S(2)}) copy-start(bf16[64,640]{1,0:T(8,128)(2,1)} %param.16) | copy-start | bytes 245764
  218.9 114.6 %all-reduce.9.cloned.1.call-start = ((), (), s32[]{:S(2)}) async-start(), calls=%async_computation.6 | async-start | bytes 3145728 | tf_op jit(solution)/shard_map/psum | solution.py:61
  239.5 51.2 %copy-start.2 = (bf16[64,640]{1,0:T(8,128)(2,1)}, bf16[64,640]{1,0:T(8,128)(2,1)S(1)}, u32[]{:S(2)}) copy-start(bf16[64,640]{1,0:T(8,128)(2,1)S(1)} %add_convert_fusion) | copy-start | bytes 245764
  284.1 49.5 %copy-start.5 = (f32[3072]{0:T(1024)S(1)}, f32[3072]{0:T(1024)}, u32[]{:S(2)}) copy-start(f32[3072]{0:T(1024)} %param.19) | copy-start | bytes 36868
  290.7 117.1 %copy-start.6 = (f32[1280]{0:T(1024)S(1)}, f32[1280]{0:T(1024)}, u32[]{:S(2)}) copy-start(f32[1280]{0:T(1024)} %param.21) | copy-start | bytes 15364
  290.7 117.1 %reduce-scatter.5.cloned.1.call-start = ((), (), s32[]{:S(2)}) async-start(), calls=%async_computation.7 | async-start | bytes 1474560 | tf_op jit(solution)/shard_map/reduce_scatter | solution.py:64
  342.4 147.5 %all-reduce.11.cloned.1.call-start = ((), (), s32[]{:S(2)}) async-start(), calls=%async_computation.8 | async-start | bytes 3145728 | tf_op jit(solution)/shard_map/psum | solution.py:83
  440.8 0.8 copy-start.1
Sparse Core Ops, SparseCore 0:
  60.8 60.2 all-reduce.4
  123.4 87.1 all-reduce.6
  219.1 19.4 reduce-scatter.2
  290.8 42.7 all-reduce.8
  342.5 65.1 reduce-scatter.4
  448.4 41.4 all-reduce.10
